TPU v7x, 256 devices: a whole 4x4x8 slice. The times are simulated.
256 devices in a mesh: dp: 8 (over z), expert: 32 (over y, x, core).
Axes of the slice: x: 4, y: 4, z: 8, core: 2. Of those that a mesh axis runs over, the one named last changes fastest.
Arguments:
- tokens: bfloat16 [65536, 1280], P(('dp', 'expert')), may hold values from -14 to 14
- ln_gain: float32 [1280], replicated, may hold values from 0.25 to 1.75
- router: bfloat16 [1280, 32], replicated, may hold values from -0.3125 to 0.3125
- w_in: bfloat16 [32, 5120, 1280], P('expert', 'dp'), may hold values from -0.15625 to 0.15625
- b_in: bfloat16 [32, 5120], P('expert', 'dp'), may hold values from -3 to 3
- w_out: bfloat16 [32, 5120, 1280], P('expert', 'dp'), may hold values from -0.078125 to 0.078125
- b_out: bfloat16 [32, 1280], P('expert'), may hold values from -3 to 3
- expert_choice: int32 [65536], P(('dp', 'expert')), may hold values from 0 to 31
- modality: int32 [65536], P(('dp', 'expert')), may hold values from 0 to 1, as said below
- slot: int32 [65536], P(('dp', 'expert')), may hold values from -1 to 15, as said below
Outputs:
- moe_out: bfloat16 [65536, 1280], P(('dp', 'expert'))
- aux_losses: float32 [2, 2], replicated
Inputs may be any that keep to these rules, and one draw needn't show every extreme that they name: Each source's tokens with one expert and a slot other than -1 have distinct slots, numbered from 0 in token order; one expert has all 16 slots filled in every source. `modality`: every source holds tokens of both modalities.
All inputs are finite; a program needn't handle non-finite values.
Results may differ from a plain program's by a relative error of at most 0.007.
Values may be sent and summed in bfloat16 or wider, within the bound.
A program may use at most 128 MiB of HBM per device.

v0:
```python
import functools

import jax
import jax.numpy as jnp
from jax import lax
from jax.sharding import Mesh
from jax.sharding import PartitionSpec as P

CAP = 16
EXPERT = ("expert_0", "expert_1", "expert_2")
DP_EXPERT = ("dp", "expert_0", "expert_1", "expert_2")


def by_axis(x, axes):
    return functools.reduce(lax.psum, axes, x)


def layer_norm(tokens, ln_gain):
    values = tokens.astype(jnp.float32)
    center = values - jnp.mean(values, axis=-1, keepdims=True)
    spread = jnp.mean(center * center, axis=-1, keepdims=True)
    return (center * lax.rsqrt(spread + 1e-06) * ln_gain).astype(jnp.bfloat16)


def expert_hidden(rows, first, first_bias, second):
    pre = lax.dot_general(rows, first, (((1,), (1,)), ((), ())), preferred_element_type=jnp.float32)
    hidden = jax.nn.gelu(pre + first_bias.astype(jnp.float32), approximate=False).astype(
        jnp.bfloat16
    )
    return jnp.dot(hidden, second, preferred_element_type=jnp.float32)


def on_device(tokens, ln_gain, router, w_in, b_in, w_out, b_out, expert_choice, modality, slot):
    normed = layer_norm(tokens, ln_gain)
    logits = jnp.dot(normed, router, preferred_element_type=jnp.float32)
    logp = jax.nn.log_softmax(logits, axis=-1)
    probs = jnp.exp(logp)
    gate = jnp.take_along_axis(probs, expert_choice[:, None], axis=1)[:, 0]
    experts_all = router.shape[1]
    width = normed.shape[1]
    columns = experts_all * CAP
    target = jnp.where(slot >= 0, expert_choice * CAP + slot, -1)
    table = (target[:, None] == jnp.arange(columns, dtype=jnp.int32)[None, :]).astype(jnp.bfloat16)
    buffer = jnp.einsum("tk,td->kd", table, normed, preferred_element_type=jnp.float32).astype(
        jnp.bfloat16
    )
    received = lax.all_to_all(
        buffer.reshape(experts_all, CAP, width), EXPERT, split_axis=0, concat_axis=0, tiled=True
    )
    senders = lax.axis_size(EXPERT)
    local_count = w_in.shape[0]
    received = received.reshape(senders, local_count, CAP, width)
    rows = received[:, 0].reshape(senders * CAP, width)
    summed = expert_hidden(
        rows,
        lax.all_gather(w_in[0], "dp", axis=0, tiled=True),
        lax.all_gather(b_in[0], "dp", axis=0, tiled=True),
        lax.all_gather(w_out[0], "dp", axis=0, tiled=True),
    )
    results = [
        (summed + b_out[0].astype(jnp.float32)).astype(jnp.bfloat16).reshape(senders, CAP, width)
    ]
    outputs = jnp.stack(results, axis=1).reshape(experts_all, CAP, width)
    returned = lax.all_to_all(outputs, EXPERT, split_axis=0, concat_axis=0, tiled=True)
    fetched = jnp.dot(table, returned.reshape(columns, width), preferred_element_type=jnp.float32)
    moe_out = (gate[:, None] * fetched).astype(jnp.bfloat16)
    textual = (modality == 1).astype(jnp.float32)
    select = jnp.stack([1.0 - textual, textual], axis=0)
    entropy = -jnp.sum(probs * logp, axis=-1)
    prob_part = jnp.dot(select, probs, precision=lax.Precision.HIGHEST)
    ent_part = jnp.dot(select, entropy, precision=lax.Precision.HIGHEST)
    count_part = jnp.sum(select, axis=1)
    prob_sum, ent_sum, count = (
        by_axis(prob_part, DP_EXPERT),
        by_axis(ent_part, DP_EXPERT),
        by_axis(count_part, DP_EXPERT),
    )
    pbar = prob_sum / count[:, None]
    aux_losses = jnp.stack([ent_sum / count, jnp.sum(pbar * jnp.log(pbar), axis=1)], axis=1)
    return (moe_out, aux_losses)


def solution(mesh):
    finer = Mesh(
        mesh.devices.reshape(mesh.shape["dp"], 4, 4, 2), ("dp", "expert_0", "expert_1", "expert_2")
    )
    return jax.shard_map(
        on_device,
        mesh=finer,
        in_specs=(
            P(DP_EXPERT, None),
            P(),
            P(),
            P(EXPERT, "dp", None),
            P(EXPERT, "dp"),
            P(EXPERT, "dp", None),
            P(EXPERT, None),
            P(DP_EXPERT),
            P(DP_EXPERT),
            P(DP_EXPERT),
        ),
        out_specs=(P(DP_EXPERT, None), P()),
        check_vma=False,
    )
```

profile of v0, /device:TPU:1, one launch (start us, length us, event | category | flops | bytes accessed | tf_op | source)
XLA Modules:
  0.0 363.0 jit_solution(15232666370423474647)
XLA Ops:
  7.3 0.7 all-gather.6.cloned.1.call-update
  8.0 0.7 all-gather.8.cloned.1.call-update
  8.7 1.3 convert_reduce_fusion
  10.0 1.4 fusion.62
  11.4 0.7 compare_select_fusion
  12.1 2.9 convolution_convert_fusion
  15.0 8.6 %all-to-all-start = ((bf16[32,16,1280]{2,1,0:T(8,128)(2,1)}), bf16[32,16,1280]{2,1,0:T(8,128)(2,1)S(1)}, u32[]{:S(2)}, u32[]{:S(2)}) async-start(bf16[32,16,1280]{2,1,0:T(8,128)(2,1)} %bitcast.3), calls=%async_computation | async-start | bytes 2621440 | tf_op jit(solution)/shard_map/all_to_all | solution.py:47
  23.6 1.5 fusion.106
  25.2 25.4 %all-gather.1 = bf16[1,5120]{1,0:T(2,128)(2,1)S(1)} all-gather(bf16[1,640]{1,0:T(2,128)(2,1)S(1)} %copy-done.4), channel_id=3, replica_groups=mesh['dp'=8,'expert_0'=4,'expert_1'=4,'expert_2'=2] {'dp'}, dimensions={1}, use_global_device_ids=true | all-gather | bytes 11520 | tf_op jit(solution)/shard_map/all_gather | solution.py:57
  50.7 101.4 %all-gather.6.cloned.1.call-done = bf16[1,5120,1280]{2,1,0:T(8,128)(2,1)} async-done(((bf16[1,640,1280]{2,1,0:T(8,128)(2,1)}), bf16[1,5120,1280]{2,1,0:T(8,128)(2,1)}) %all-gather.6.cloned.1.call-update) | async-done | bytes 13107216 | tf_op jit(solution)/shard_map/all_gather | solution.py:56
  152.1 31.7 %fusion.6.clone.8 = bf16[512,5120]{1,0:T(8,128)(2,1)} fusion(bf16[512,1280]{1,0:T(8,128)(2,1)S(1)} %bitcast.49, bf16[1,5120,1280]{2,1,0:T(8,128)(2,1)} %all-gather.6.cloned.1.call-done, f32[5120]{0:T(1024)S(1)} %bitcast.50), kind=kOutput, calls=%fused_computation.8.clone.clone.clone.clone.clone.clone.clone.1 | convolution fusion | flops 6883901440 | bytes 19681280 | tf_op jit(solution)/shard_map/dot_general | solution.py:26
  183.8 106.9 %all-gather.8.cloned.1.call-done = bf16[1,5120,1280]{2,1,0:T(8,128)(2,1)} async-done(((bf16[1,640,1280]{2,1,0:T(8,128)(2,1)}), bf16[1,5120,1280]{2,1,0:T(8,128)(2,1)}) %all-gather.8.cloned.1.call-update) | async-done | bytes 13107216 | tf_op jit(solution)/shard_map/all_gather | solution.py:58
  290.8 13.5 %fusion.54 = bf16[512,1280]{1,0:T(8,128)(2,1)} fusion(bf16[1,5120,1280]{2,1,0:T(8,128)(2,1)} %all-gather.8.cloned.1.call-done, f32[1280]{0:T(1024)S(1)} %convert_reduce_fusion.1, bf16[512,5120]{1,0:T(8,128)(2,1)} %fusion.6.clone.8), kind=kOutput, calls=%fused_computation.57 | convolution fusion | flops 6712197120 | bytes 19665920 | tf_op jit(solution)/shard_map/dot_general | solution.py:30
  304.2 7.7 %all-to-all-start.1 = ((bf16[32,16,1280]{2,1,0:T(8,128)(2,1)}), bf16[32,16,1280]{2,1,0:T(8,128)(2,1)S(1)}, u32[]{:S(2)}, u32[]{:S(2)}) async-start(bf16[32,16,1280]{2,1,0:T(8,128)(2,1)} %bitcast.8), calls=%async_computation.1 | async-start | bytes 2621440 | tf_op jit(solution)/shard_map/all_to_all | solution.py:64
  311.9 0.1 convolution_bitcast_fusion
  312.2 0.1 fusion.67
  312.3 12.9 %all-reduce = (f32[2,32]{1,0:T(2,128)S(1)}, f32[2]{0:T(128)S(1)}, f32[2]{0:T(128)S(1)}) all-reduce(f32[2,32]{1,0:T(2,128)S(1)} %fusion.67, f32[2]{0:T(128)S(1)} %fusion.102, f32[2]{0:T(128)S(1)} %convolution_bitcast_fusion), channel_id=1, replica_groups=mesh['dp'=8,'expert_0'=4,'expert_1'=4,'expert_2'=2] {'dp'}, use_global_device_ids=true, to_apply=%region_14.15 | all-reduce | flops 68 | bytes 544 | tf_op jit(solution)/shard_map/psum | solution.py:15
  325.3 8.6 %all-reduce.2 = (f32[2,32]{1,0:T(2,128)S(1)}, f32[2]{0:T(128)S(1)}, f32[2]{0:T(128)S(1)}) all-reduce(f32[2,32]{1,0:T(2,128)S(1)} %get-tuple-element.8, f32[2]{0:T(128)S(1)} %get-tuple-element.9, f32[2]{0:T(128)S(1)} %get-tuple-element.10), channel_id=1, replica_groups=mesh['dp'=8,'expert_0'=4,'expert_1'=4,'expert_2'=2] {'expert_0'}, use_global_device_ids=true, to_apply=%region_15.16 | all-reduce | flops 68 | bytes 544 | tf_op jit(solution)/shard_map/psum | solution.py:15
  333.9 8.4 %all-reduce.1 = (f32[2,32]{1,0:T(2,128)S(1)}, f32[2]{0:T(128)S(1)}, f32[2]{0:T(128)S(1)}) all-reduce(f32[2,32]{1,0:T(2,128)S(1)} %get-tuple-element.14, f32[2]{0:T(128)S(1)} %get-tuple-element.15, f32[2]{0:T(128)S(1)} %get-tuple-element.16), channel_id=1, replica_groups=mesh['dp'=8,'expert_0'=4,'expert_1'=4,'expert_2'=2] {'expert_1'}, use_global_device_ids=true, to_apply=%region_16.17 | all-reduce | flops 68 | bytes 544 | tf_op jit(solution)/shard_map/psum | solution.py:15
  342.3 9.1 %all-reduce.3 = (f32[2,32]{1,0:T(2,128)S(1)}, f32[2]{0:T(128)S(1)}, f32[2]{0:T(128)S(1)}) all-reduce(f32[2,32]{1,0:T(2,128)S(1)} %get-tuple-element.11, f32[2]{0:T(128)S(1)} %get-tuple-element.12, f32[2]{0:T(128)S(1)} %get-tuple-element.13), channel_id=1, replica_groups=mesh['dp'=8,'expert_0'=4,'expert_1'=4,'expert_2'=2] {'expert_2'}, use_global_device_ids=true, to_apply=%region_17.18 | all-reduce | flops 68 | bytes 544 | tf_op jit(solution)/shard_map/psum | solution.py:15
  351.4 0.2 fusion.68
  351.6 0.7 copy.14
  352.3 2.4 gather_fusion
  354.7 1.4 fusion.59
  (31 shorter events, 0.4 us)
Async XLA Ops:
  7.2 16.4 %copy-start = (bf16[1280,32]{0,1:T(8,128)(2,1)S(1)}, bf16[1280,32]{0,1:T(8,128)(2,1)}, u32[]{:S(2)}) copy-start(bf16[1280,32]{0,1:T(8,128)(2,1)} %param.12) | copy-start | bytes 245764
  7.2 18.0 %copy-start.4 = (bf16[1,640]{1,0:T(2,128)(2,1)S(1)}, bf16[1,640]{1,0:T(2,128)(2,1)}, u32[]{:S(2)}) copy-start(bf16[1,640]{1,0:T(2,128)(2,1)} %param.14) | copy-start | bytes 3844
  7.2 43.4 %copy-start.1 = (bf16[1,1280]{1,0:T(2,128)(2,1)S(1)}, bf16[1,1280]{1,0:T(2,128)(2,1)}, u32[]{:S(2)}) copy-start(bf16[1,1280]{1,0:T(2,128)(2,1)} %param.16) | copy-start | bytes 7684
  7.2 43.5 %copy-start.2 = (s32[256]{0:T(256)S(1)}, s32[256]{0:T(256)}, u32[]{:S(2)}) copy-start(s32[256]{0:T(256)} %param.18) | copy-start | bytes 3076
  7.2 144.9 %all-gather.6.cloned.1.call-start = ((), (), s32[]{:S(2)}) async-start(), calls=%async_computation.2 | async-start | bytes 14745600 | tf_op jit(solution)/shard_map/all_gather | solution.py:56
  7.9 282.8 %all-gather.8.cloned.1.call-start = ((), (), s32[]{:S(2)}) async-start(), calls=%async_computation.3 | async-start | bytes 14745600 | tf_op jit(solution)/shard_map/all_gather | solution.py:58
  15.0 35.7 %all-to-all-start = ((bf16[32,16,1280]{2,1,0:T(8,128)(2,1)}), bf16[32,16,1280]{2,1,0:T(8,128)(2,1)S(1)}, u32[]{:S(2)}, u32[]{:S(2)}) async-start(bf16[32,16,1280]{2,1,0:T(8,128)(2,1)} %bitcast.3), calls=%async_computation | async-start | bytes 2621440 | tf_op jit(solution)/shard_map/all_to_all | solution.py:47
  183.8 170.9 %copy-start.3 = (s32[256]{0:T(256)S(1)}, s32[256]{0:T(256)}, u32[]{:S(2)}) copy-start(s32[256]{0:T(256)} %param.17) | copy-start | bytes 3076
  304.2 50.5 %all-to-all-start.1 = ((bf16[32,16,1280]{2,1,0:T(8,128)(2,1)}), bf16[32,16,1280]{2,1,0:T(8,128)(2,1)S(1)}, u32[]{:S(2)}, u32[]{:S(2)}) async-start(bf16[32,16,1280]{2,1,0:T(8,128)(2,1)} %bitcast.8), calls=%async_computation.1 | async-start | bytes 2621440 | tf_op jit(solution)/shard_map/all_to_all | solution.py:64
Sparse Core Ops, SparseCore 0:
  9.8 142.2 all-gather.5
  153.9 136.8 all-gather.7
where the time goes:
time: 363 us
  waiting for transfers between devices  210 us (58%)
  blocking collectives  64.5 us (18%)
  matrix products  51.3 us (14%)
  starting transfers between devices  16.4 us (5%)
  between operations  14.2 us (4%)
  other arithmetic  3.85 us (1%)
    all_gather x1, waiting for transfers between devices, on_device(): lax.all_gather(w_out[0], 'dp', axis=0, tiled=True)  107 us
    all_gather x1, waiting for transfers between devices, on_device(): lax.all_gather(w_in[0], 'dp', axis=0, tiled=True)  101 us
    psum x4, blocking collectives, by_axis(): return functools.reduce(lax.psum, axes, x)  39.1 us
    dot_general x1, matrix products, expert_hidden(): lax.dot_general(rows, first, (((1,), (1,)), ((), ())), preferred_element_...  31.7 us
    all_gather x1, blocking collectives, on_device(): lax.all_gather(b_in[0], 'dp', axis=0, tiled=True)  25.4 us
    dot_general x1, matrix products, expert_hidden(): return jnp.dot(hidden, second, preferred_element_type=jnp.float32)  13.5 us
    all_to_all x1, starting transfers between devices, on_device(): lax.all_to_all(buffer.reshape(experts_all, CAP, width), EXPERT, split_axi...  8.58 us
    all_to_all x1, starting transfers between devices, on_device(): lax.all_to_all(outputs, EXPERT, split_axis=0, concat_axis=0, tiled=True)  7.7 us
  transfers between devices with their start and end apart: 4, of which 2 were waited for; matrix products, arithmetic and copies ran while one was open for 12% of the time, Pallas kernels for 0%

commit v1 on v0

v1 whole, which is shorter than its diff:
```python
import functools

import jax
import jax.numpy as jnp
from jax import lax
from jax.experimental import pallas as pl
from jax.experimental.pallas import tpu as pltpu
from jax.sharding import Mesh
from jax.sharding import PartitionSpec as P

CAP = 16
DP, EY, EX = "dp", "expert_y", "expert_x"
EXPERT = (EY, EX)
DP_EXPERT = (DP, EY, EX)
MESH = pl.DeviceIdType.MESH
REL = (0, 1, 3, 2)
N = 8


def layer_norm(tokens, ln_gain):
    values = tokens.astype(jnp.float32)
    center = values - jnp.mean(values, axis=-1, keepdims=True)
    spread = jnp.mean(center * center, axis=-1, keepdims=True)
    return (center * lax.rsqrt(spread + 1e-06) * ln_gain).astype(jnp.bfloat16)


def gelu(x):
    return 0.5 * x * (1.0 + lax.erf(x * 0.7071067811865476))


def kernel(
    ny,
    nx,
    buf,
    w_in,
    b_in,
    w_out,
    b_out,
    stats,
    ret,
    tot,
    rows,
    recvm,
    recvp,
    partm,
    partp,
    own,
    ps,
    outb,
    statz,
    statp,
    a_send,
    a_recv,
    gp_recv,
    gm_recv,
    g_send,
    rp_recv,
    rm_recv,
    r_send,
    o_send,
    o_recv,
    s_send,
    s_recv,
):
    rc = nx * CAP
    rb = ny * rc
    z, y, x = lax.axis_index(DP), lax.axis_index(EY), lax.axis_index(EX)
    up, down = lax.rem(z + 1, N), lax.rem(z + N - 1, N)
    expert = y * nx + x

    def at(z_to, y_to, x_to):
        return {DP: z_to, EY: y_to, EX: x_to}

    def send(src, dst, ssem, rsem, to):
        copy = pltpu.make_async_remote_copy(
            src_ref=src, dst_ref=dst, send_sem=ssem, recv_sem=rsem, device_id=to, device_id_type=MESH
        )
        copy.start()

    def arrived(dst, rsem):
        pltpu.make_async_copy(dst, dst, rsem).wait()

    barrier = pltpu.get_barrier_semaphore()

    @pl.loop(1, N)
    def _(k):
        pl.semaphore_signal(barrier, inc=1, device_id=at(lax.rem(z + k, N), y, x), device_id_type=MESH)

    @pl.loop(1, ny * nx)
    def _(k):
        other = lax.rem(expert + k, ny * nx)
        pl.semaphore_signal(
            barrier, inc=1, device_id=at(z, lax.div(other, nx), lax.rem(other, nx)), device_id_type=MESH
        )

    pl.semaphore_wait(barrier, N - 1 + ny * nx - 1)

    mine = pl.ds(pl.multiple_of(x * CAP, CAP), CAP)
    rows[mine, :] = buf[pl.ds(pl.multiple_of(expert * CAP, CAP), CAP), :]
    for c in range(ny):
        y_to = lax.rem(y + ny - REL[c], ny)
        spot = pl.ds(pl.multiple_of(c * rc + x * CAP, CAP), CAP)

        @pl.loop(0 if c else 1, nx)
        def _(k):
            x_to = lax.rem(x + k, nx)
            src = pl.ds(pl.multiple_of((y_to * nx + x_to) * CAP, CAP), CAP)
            send(buf.at[src], rows.at[spot], a_send.at[c], a_recv.at[c], at(z, y_to, x_to))

    statz[0] = stats[...]

    @pl.loop(1, N)
    def _(k):
        send(stats, statz.at[k], s_send.at[0], s_recv.at[0], at(lax.rem(z + k, N), y, x))

    def chunk(d, c):
        return pl.ds(pl.multiple_of(d * rb + c * rc, CAP), rc)

    def gather_up(d, c):
        send(rows.at[chunk(d, c)], rows.at[chunk(d + 1, c)], g_send.at[0], gp_recv.at[d + 1, c], at(up, y, x))

    def gather_down(d, c):
        src = d % N
        send(rows.at[chunk(src, c)], rows.at[chunk(d - 1, c)], g_send.at[1], gm_recv.at[d - 1, c], at(down, y, x))

    def have_up(d, c):
        arrived(rows.at[chunk(d, c)], gp_recv.at[d, c])

    def have_down(d, c):
        arrived(rows.at[chunk(d, c)], gm_recv.at[d, c])

    def ffn(xs):
        pre = lax.dot_general(xs, w_in[...], (((1,), (1,)), ((), ())), preferred_element_type=jnp.float32)
        hidden = gelu(pre + b_in[...]).astype(jnp.bfloat16)
        return jnp.dot(hidden, w_out[...], preferred_element_type=jnp.float32)

    for p in range(2):
        a, b = 2 * p, 2 * p + 1
        for c in (a, b):
            n_in = rc if c else rc - CAP
            arrived(rows.at[pl.ds(c * rc, n_in)], a_recv.at[c])
            gather_up(0, c)
            gather_down(N, c)
        for s in range(1, 4):
            for c in (a, b):
                have_up(s, c)
                if s < 3 or c == a:
                    gather_up(s, c)
                have_down(N - s, c)
                if s < 3 or c == b:
                    gather_down(N - s, c)
        if p == 0:
            have_up(4, a)
            have_down(4, b)
            total = statz[0]
            arrived(statz.at[pl.ds(1, N - 1)], s_recv.at[0])
            for k in range(1, N):
                total = total + statz[k]
            statp[0] = total

            @pl.loop(1, ny * nx)
            def _(k):
                other = lax.rem(expert + k, ny * nx)
                send(
                    statp.at[0],
                    statp.at[k],
                    s_send.at[1],
                    s_recv.at[1],
                    at(z, lax.div(other, nx), lax.rem(other, nx)),
                )

    @pl.loop(0, ny * rc // 256 if ny * rc >= 256 else 1)
    def _(k):
        m = min(256, ny * rc)
        here = pl.ds(pl.multiple_of(k * m, CAP), m)
        own[here, :] = ffn(rows[here, :])

    def finish(c):
        here = pl.ds(c * rc, rc)
        arrived(recvm.at[pl.ds(c * rc, rc)], rm_recv.at[0, c])
        arrived(recvp.at[pl.ds(3 * rb + c * rc, rc)], rp_recv.at[3, c])
        total = own[here, :] + b_out[...]
        total = total + recvm[pl.ds(c * rc, rc), :].astype(jnp.float32)
        total = total + recvp[pl.ds(3 * rb + c * rc, rc), :].astype(jnp.float32)
        outb[here, :] = total.astype(jnp.bfloat16)
        y_to = lax.rem(y + REL[c], ny)
        to = pl.ds(pl.multiple_of(expert * CAP, CAP), CAP)

        @pl.loop(0 if c else 1, nx)
        def _(k):
            x_to = lax.rem(x + k, nx)
            src = pl.ds(pl.multiple_of(c * rc + x_to * CAP, CAP), CAP)
            send(outb.at[src], ret.at[to], o_send.at[0], o_recv.at[0], at(z, y_to, x_to))

        if c == 0:
            ret[to, :] = outb[mine, :]

    @pl.loop(0, 14)
    def _(t):
        p = lax.div(t, 7)
        i = lax.rem(t, 7)
        k = lax.div(i + 1, 2)
        odd = lax.rem(i, 2)
        cm = 2 * p + odd
        cp = 2 * p + 1 - odd

        @pl.when(t == 7)
        def _():
            have_up(4, 2)
            have_down(4, 3)

        sm = chunk(4 - k, cm)
        sp = chunk(4 + k, cp)
        ps[...] = ffn(jnp.concatenate([rows[sm, :], rows[sp, :]], axis=0))
        om = chunk(4 - k, cm)
        mm = pl.ds(pl.multiple_of((3 - k) * rb + cm * rc, CAP), rc)
        pp = pl.ds(pl.multiple_of(k * rb + cp * rc, CAP), rc)

        @pl.when(i < 2)
        def _():
            partm[mm, :] = ps[pl.ds(0, rc), :].astype(jnp.bfloat16)
            partp[pp, :] = ps[pl.ds(rc, rc), :].astype(jnp.bfloat16)

        @pl.when(i >= 2)
        def _():
            got_m = pl.ds(pl.multiple_of((4 - k) * rb + cm * rc, CAP), rc)
            arrived(recvm.at[got_m], rm_recv.at[4 - k, cm])
            partm[mm, :] = (ps[pl.ds(0, rc), :] + recvm[got_m, :].astype(jnp.float32)).astype(jnp.bfloat16)
            got_p = pl.ds(pl.multiple_of((k - 1) * rb + cp * rc, CAP), rc)
            arrived(recvp.at[got_p], rp_recv.at[k - 1, cp])
            partp[pp, :] = (ps[pl.ds(rc, rc), :] + recvp[got_p, :].astype(jnp.float32)).astype(jnp.bfloat16)

        send(partm.at[mm], recvm.at[mm], r_send.at[0], rm_recv.at[3 - k, cm], at(down, y, x))
        send(partp.at[pp], recvp.at[pp], r_send.at[1], rp_recv.at[k, cp], at(up, y, x))

        @pl.when(t == 9)
        def _():
            finish(0)
            finish(1)

    total = statp[0]
    arrived(statp.at[pl.ds(1, ny * nx - 1)], s_recv.at[1])
    for k in range(1, ny * nx):
        total = total + statp[k]
    tot[...] = total
    finish(2)
    finish(3)
    arrived(ret.at[pl.ds(0, ny * rc - CAP)], o_recv.at[0])
    arrived(ret.at[pl.ds(0, ny * rc - CAP)], o_send.at[0])
    for c in range(ny):
        arrived(buf.at[pl.ds(0, rc if c else rc - CAP)], a_send.at[c])
    for k in range(2):
        arrived(rows.at[pl.ds(0, 14 * rc)], g_send.at[k])
        arrived(partm.at[pl.ds(0, 14 * rc)], r_send.at[k])
    arrived(statz.at[pl.ds(1, N - 1)], s_send.at[0])
    arrived(statp.at[pl.ds(1, ny * nx - 1)], s_send.at[1])


def exchange(ny, nx, buf, w_in, b_in, w_out, b_out, stats):
    columns, width = buf.shape
    ff = w_in.shape[0]
    rc = nx * CAP
    vmem = pl.BlockSpec(memory_space=pltpu.VMEM)
    dma = pltpu.SemaphoreType.DMA
    return pl.pallas_call(
        functools.partial(kernel, ny, nx),
        out_shape=(
            jax.ShapeDtypeStruct((columns, width), jnp.bfloat16),
            jax.ShapeDtypeStruct(stats.shape, jnp.float32),
        ),
        in_specs=[vmem] * 6,
        out_specs=(vmem, vmem),
        scratch_shapes=[
            pltpu.VMEM((N * columns, width), jnp.bfloat16),
            pltpu.VMEM((4 * columns, width), jnp.bfloat16),
            pltpu.VMEM((4 * columns, width), jnp.bfloat16),
            pltpu.VMEM((4 * columns, width), jnp.bfloat16),
            pltpu.VMEM((4 * columns, width), jnp.bfloat16),
            pltpu.VMEM((columns, width), jnp.float32),
            pltpu.VMEM((2 * rc, width), jnp.float32),
            pltpu.VMEM((columns, width), jnp.bfloat16),
            pltpu.VMEM((N,) + stats.shape, jnp.float32),
            pltpu.VMEM((ny * nx,) + stats.shape, jnp.float32),
            dma((ny,)),
            dma((ny,)),
            dma((5, ny)),
            dma((8, ny)),
            dma((2,)),
            dma((4, ny)),
            dma((4, ny)),
            dma((2,)),
            dma((1,)),
            dma((1,)),
            dma((2,)),
            dma((2,)),
        ],
        compiler_params=pltpu.CompilerParams(
            collective_id=0, has_side_effects=True, vmem_limit_bytes=60 * 1024 * 1024
        ),
    )(buf, w_in, b_in, w_out, b_out, stats)


def on_device(tokens, ln_gain, router, w_in, b_in, w_out, b_out, expert_choice, modality, slot):
    ny, nx = lax.axis_size(EY), lax.axis_size(EX)
    normed = layer_norm(tokens, ln_gain)
    logits = jnp.dot(normed, router, preferred_element_type=jnp.float32)
    logp = jax.nn.log_softmax(logits, axis=-1)
    probs = jnp.exp(logp)
    experts_all = router.shape[1]
    columns = experts_all * CAP
    picked = expert_choice[:, None] == jnp.arange(experts_all, dtype=jnp.int32)[None, :]
    gate = jnp.sum(jnp.where(picked, probs, 0.0), axis=1)
    target = jnp.where(slot >= 0, expert_choice * CAP + slot, -1)
    table = (target[:, None] == jnp.arange(columns, dtype=jnp.int32)[None, :]).astype(jnp.bfloat16)
    buffer = jnp.einsum("tk,td->kd", table, normed, preferred_element_type=jnp.float32).astype(jnp.bfloat16)

    textual = (modality == 1).astype(jnp.float32)
    select = jnp.stack([1.0 - textual, textual], axis=0)
    entropy = -jnp.sum(probs * logp, axis=-1)
    per_token = jnp.concatenate([probs, entropy[:, None], jnp.ones_like(entropy)[:, None]], axis=1)
    part = jnp.dot(select, per_token, precision=lax.Precision.HIGHEST)
    stats = jnp.pad(part, ((0, 6), (0, 128 - part.shape[1])))

    returned, total = exchange(
        ny,
        nx,
        buffer,
        w_in[0],
        b_in.astype(jnp.float32),
        w_out[0],
        b_out.astype(jnp.float32),
        stats,
    )
    fetched = jnp.dot(table, returned, preferred_element_type=jnp.float32)
    moe_out = (gate[:, None] * fetched).astype(jnp.bfloat16)
    prob_sum, ent_sum, count = total[:2, :experts_all], total[:2, experts_all], total[:2, experts_all + 1]
    pbar = prob_sum / count[:, None]
    aux_losses = jnp.stack([ent_sum / count, jnp.sum(pbar * jnp.log(pbar), axis=1)], axis=1)
    return (moe_out, aux_losses)


def solution(mesh):
    finer = Mesh(mesh.devices.reshape(mesh.shape["dp"], 4, 8), (DP, EY, EX))
    return jax.shard_map(
        on_device,
        mesh=finer,
        in_specs=(
            P(DP_EXPERT, None),
            P(),
            P(),
            P(EXPERT, DP, None),
            P(EXPERT, DP),
            P(EXPERT, DP, None),
            P(EXPERT, None),
            P(DP_EXPERT),
            P(DP_EXPERT),
            P(DP_EXPERT),
        ),
        out_specs=(P(DP_EXPERT, None), P()),
        check_vma=False,
    )
```

time: 363 us -> 255 us (0.70)
  Pallas kernels: 0 us -> 239 us
  waiting for transfers between devices: 210 us -> 0 us
  blocking collectives: 64.5 us -> 0 us
  matrix products: 51.3 us -> 5.18 us
  starting transfers between devices: 16.4 us -> 0 us
  between operations: 14.2 us -> 0.75 us
    pallas_call x0 -> x1, Pallas kernels: none -> 239 us  [exchange(): pl.pallas_call(functools.partial(kernel, ny, nx), out_shape=(jax.ShapeDty...]
    all_gather x2 -> x0, waiting for transfers between devices: 208 us -> none  [the longest x1 107 us: on_device(): lax.all_gather(w_out[0], 'dp', axis=0, tiled=True)]
    dot_general x5 -> x2, matrix products: 46.9 us -> 2.9 us  [the longest x1 2.7 us: on_device(): fetched = jnp.dot(table, returned, preferred_element_type=jnp.float32)]
    psum x4 -> x0, blocking collectives: 39.1 us -> none  [by_axis(): return functools.reduce(lax.psum, axes, x)]
    all_gather x1 -> x0, blocking collectives: 25.4 us -> none  [on_device(): lax.all_gather(b_in[0], 'dp', axis=0, tiled=True)]
    all_to_all x2 -> x0, starting transfers between devices: 16.3 us -> none  [the longest x1 8.58 us: on_device(): lax.all_to_all(buffer.reshape(experts_all, CAP, width), EXPERT, split_axi...]
  transfers between devices with their start and end apart: 4 -> 0, of which waited for: 2 -> 0; matrix products, arithmetic and copies ran while one was open for 12% -> 0% of each run, Pallas kernels for 0% -> 0%
where the time goes in v1:
time: 255 us; the launch traced here: 253 us
  Pallas kernels  239 us (94%)
  other arithmetic  7.13 us (3%)
  matrix products  5.18 us (2%)
    pallas_call x1, Pallas kernels, exchange(): pl.pallas_call(functools.partial(kernel, ny, nx), out_shape=(jax.ShapeDty...  239 us

profile of v1, /device:TPU:1, one launch (start us, length us, event | category | flops | bytes accessed | tf_op | source)
XLA Modules:
  0.0 252.8 jit_solution(10101026527328913178)
XLA Ops:
  0.6 0.0 copy-start
  0.6 0.0 copy-start.1
  0.7 0.0 copy-start.6
  0.7 0.0 copy-start.2
  0.7 0.1 pad.9.clone
  0.8 0.8 compare_select_fusion
  1.6 0.7 broadcast_subtract_fusion
  2.3 0.7 compare_convert_fusion
  2.9 1.3 convert_reduce_fusion
  4.2 1.4 fusion.3
  5.6 0.6 convert_element_type.27.b_in
  6.2 0.0 copy-done.2
  6.2 0.6 convert_element_type.28.b_out
  6.8 0.4 fusion.22
  7.4 0.2 fusion.8
  7.6 0.6 pad.4.stats
  8.2 1.8 convolution_convert_fusion.buf
  10.0 238.9 %shard_map.113 = (bf16[512,1280]{1,0:T(8,128)(2,1)}, f32[8,128]{1,0:T(8,128)}) custom-call(bf16[512,1280]{1,0:T(8,128)(2,1)} %convolution_convert_fusion.buf, bf16[640,1280]{1,0:T(8,128)(2,1)} %bitcast.9, f32[1,640]{1,0:T(1,128)} %convert_element_type.27.b_in, bf16[640,1280]{1,0:T(8,128)(2,1)} %bitcast.10, f32[1,1280]{1,0:T(1,128)} %convert_element_type.28.b_out, ...), custom_call_target="tpu_custom_call" | custom-call | tf_op jit(solution)/shard_map/pallas_call | solution.py:265
  248.9 2.7 %fusion = bf16[256,1280]{1,0:T(8,128)(2,1)} fusion(bf16[512,1280]{1,0:T(8,128)(2,1)} %get-tuple-element.4, f32[256]{0:T(256)S(1)} %get-tuple-element.6, s32[256]{0:T(256)S(1)} %compare_select_fusion), kind=kOutput, calls=%fused_computation.2 | convolution fusion | flops 336330752 | bytes 1968128 | tf_op jit(solution)/shard_map/dot_general | solution.py:334
  251.6 0.0 copy-done.5
  251.6 0.2 slice_divide_fusion
  251.8 0.2 fusion.17
  252.0 0.1 copy.13
  252.1 0.7 pad_maximum_fusion
  (14 shorter events, 0.1 us)
Async XLA Ops:
  0.6 6.2 %copy-start = (bf16[1280,32]{0,1:T(8,128)(2,1)S(1)}, bf16[1280,32]{0,1:T(8,128)(2,1)}, u32[]{:S(2)}) copy-start(bf16[1280,32]{0,1:T(8,128)(2,1)} %param.12) | copy-start | bytes 245764
  0.6 6.2 %copy-start.1 = (bf16[256,1280]{1,0:T(8,128)(2,1)S(1)}, bf16[256,1280]{1,0:T(8,128)(2,1)}, u32[]{:S(2)}) copy-start(bf16[256,1280]{1,0:T(8,128)(2,1)} %param.10) | copy-start | bytes 1966084
  0.7 6.2 %copy-start.6 = (f32[1280]{0:T(1024)S(1)}, f32[1280]{0:T(1024)}, u32[]{:S(2)}) copy-start(f32[1280]{0:T(1024)} %param.11) | copy-start | bytes 15364
  0.7 5.6 %copy-start.2 = (bf16[1,1280]{1,0:T(2,128)(2,1)S(1)}, bf16[1,1280]{1,0:T(2,128)(2,1)}, u32[]{:S(2)}) copy-start(bf16[1,1280]{1,0:T(2,128)(2,1)} %param.16) | copy-start | bytes 7684
  0.7 4.9 %copy-start.4 = (bf16[1,640]{1,0:T(2,128)(2,1)S(1)}, bf16[1,640]{1,0:T(2,128)(2,1)}, u32[]{:S(2)}) copy-start(bf16[1,640]{1,0:T(2,128)(2,1)} %param.14) | copy-start | bytes 3844
  2.9 4.4 %copy-start.3 = (s32[256]{0:T(256)S(1)}, s32[256]{0:T(256)}, u32[]{:S(2)}) copy-start(s32[256]{0:T(256)} %param.17) | copy-start | bytes 3076
  248.9 2.7 %copy-start.5 = (f32[8,128]{1,0:T(8,128)S(1)}, f32[8,128]{1,0:T(8,128)}, u32[]{:S(2)}) copy-start(f32[8,128]{1,0:T(8,128)} %get-tuple-element.5) | copy-start | bytes 12292
